TPU v7x, 32 devices: a whole 2x2x4 slice. The times are simulated.
32 devices in a mesh: group: 2 (over y), expert: 4 (over x, core), tensor: 4 (over z).
Axes of the slice: x: 2, y: 2, z: 4, core: 2. Of those that a mesh axis runs over, the one named last changes fastest.
Arguments:
- tokens: bfloat16 [512, 4096], P(('group', 'expert'), 'tensor'), parts along dimension 0, may hold values from -6 to 6
- w_gate: bfloat16 [8, 4096, 1536], P('expert', 'tensor'), may hold values from -0.125 to 0.125
- w_up: bfloat16 [8, 4096, 1536], P('expert', 'tensor'), may hold values from -0.125 to 0.125
- w_down: bfloat16 [8, 1536, 4096], P('expert', None, 'tensor'), may hold values from -0.15625 to 0.15625
- expert_ids: int32 [512, 8], P(('group', 'expert')), parts along dimension 0, may hold values from 0 to 7, as said below
- route_weights: float32 [512, 8], P(('group', 'expert')), parts along dimension 0, may hold values from 0.05 to 0.5
Outputs:
- mixed_out: bfloat16 [512, 4096], P(('group', 'expert'), 'tensor'), parts along dimension 0
There are 2 independent parts, one for each index of `group`. A program takes and returns all parts, laid end to end along the dimension named above; an argument that names none is the same for every part. Nothing has to cross between parts.
Inputs may be any that keep to these rules, and one draw needn't show every extreme that they name: `expert_ids`: each row names 8 different experts. In each aligned block of 64 rows no expert is named by more than 64 rows, and one expert, the same in every block of a part, is named by exactly 64 rows of every block.
All inputs are finite; a program needn't handle non-finite values.
Results may differ from a plain program's by a relative error of at most 0.0057.
Values may be sent and summed in bfloat16 or wider, within the bound.
A program may use at most 128 MiB of HBM per device.

v0:
```python
import jax
import jax.numpy as jnp
from jax import lax
from jax.sharding import PartitionSpec as P


def slot_numbers(flat_ids, experts_all):
    labels = jnp.arange(experts_all, dtype=jnp.int32)
    onehot = (flat_ids[:, None] == labels[None, :]).astype(jnp.int32)
    before = jnp.cumsum(onehot, axis=0) - onehot
    return jnp.sum(before * onehot, axis=1)


def per_device(tokens, w_gate, w_up, w_down, expert_ids, route_weights):
    n_expert = lax.axis_size("expert")
    held_experts = w_gate.shape[0]
    experts_all = held_experts * n_expert
    tok_rows = tokens.shape[0]
    col_share = tokens.shape[1]
    per_token = expert_ids.shape[1]
    capacity = min(tok_rows, 2 * tok_rows * per_token // experts_all)
    flat_ids = expert_ids.reshape(tok_rows * per_token)
    position = flat_ids * capacity + slot_numbers(flat_ids, experts_all)
    owners = jnp.arange(tok_rows * per_token, dtype=jnp.int32) // per_token
    source = jnp.full((experts_all * capacity,), -1, jnp.int32).at[position].set(owners)
    filled = (source >= 0)[:, None]
    picked_rows = jnp.where(filled, tokens[jnp.maximum(source, 0)], jnp.zeros((), tokens.dtype))
    outgoing = picked_rows.reshape(n_expert, held_experts, capacity, col_share)
    received = lax.all_to_all(outgoing, "expert", split_axis=0, concat_axis=0, tiled=True)
    gate_part = jnp.einsum("sjnd,jdf->sjnf", received, w_gate, preferred_element_type=jnp.float32)
    up_part = jnp.einsum("sjnd,jdf->sjnf", received, w_up, preferred_element_type=jnp.float32)
    gate_share = lax.psum_scatter(gate_part, "tensor", scatter_dimension=3, tiled=True)
    up_share = lax.psum_scatter(up_part, "tensor", scatter_dimension=3, tiled=True)
    hidden_share = (jax.nn.silu(gate_share) * up_share).astype(jnp.bfloat16)
    hidden = lax.all_gather(hidden_share, "tensor", axis=3, tiled=True)
    result = jnp.einsum("sjnf,jfd->sjnd", hidden, w_down, preferred_element_type=jnp.float32)
    returned = result.astype(jnp.bfloat16)
    combined = lax.all_to_all(returned, "expert", split_axis=0, concat_axis=0, tiled=True).reshape(
        experts_all * capacity, col_share
    )
    picked = combined[position].reshape(tok_rows, per_token, col_share).astype(jnp.float32)
    mixed_out = jnp.sum(picked * route_weights[:, :, None], axis=1)
    return mixed_out.astype(jnp.bfloat16)


def solution(mesh):
    in_specs = (
        P(("group", "expert"), "tensor"),
        P("expert", "tensor", None),
        P("expert", "tensor", None),
        P("expert", None, "tensor"),
        P(("group", "expert"), None),
        P(("group", "expert"), None),
    )
    out_specs = P(("group", "expert"), "tensor")
    return jax.shard_map(
        per_device, mesh=mesh, in_specs=in_specs, out_specs=out_specs, check_vma=False
    )
```

profile of v0, /device:TPU:0, one launch (start us, length us, event | category | flops | bytes accessed | tf_op | source)
XLA Modules:
  0.0 236.0 jit_solution(6427868677075579159)
XLA Ops:
  6.5 0.0 copy-start
  6.5 0.0 reduce-scatter.3.cloned.1.call-start
  6.5 0.8 copy.16
  7.3 0.1 eq.29
  7.4 0.1 eq.25
  7.5 0.7 broadcast_multiply_fusion
  8.2 1.1 reduce-window.6
  9.4 0.2 slice_reduce_fusion
  9.6 0.1 copy.15
  9.7 0.1 mul.32
  9.8 0.1 fusion.22
  9.9 2.4 %scatter_custom_fusion = s32[512]{0:T(512)S(1)} fusion(s32[512]{0:T(512)S(1)} %bitcast.47, s32[512]{0:T(512)S(1)} %add_select_fusion, s32[]{:T(128)} %constant.27.clone.1), kind=kCustom, calls=%fused_computation.39 | custom fusion | bytes 2052 | tf_op jit(solution)/shard_map/scatter | solution.py:25
  12.4 0.1 broadcast_in_dim.26
  12.5 0.0 copy-done
  12.5 2.1 gather_fusion
  14.5 0.1 broadcast_select_fusion
  14.7 18.5 %all_to_all.10 = bf16[4,2,64,1024]{3,2,1,0:T(8,128)(2,1)S(1)} all-to-all(bf16[4,2,64,1024]{3,2,1,0:T(8,128)(2,1)S(1)} %broadcast_select_fusion), channel_id=1, replica_groups=mesh['group'=2,'expert'=4,'tensor'=4] {'expert'}, dimensions={0} | all-to-all | bytes 2097152 | tf_op jit(solution)/shard_map/all_to_all | solution.py:29
  33.2 6.3 %fusion.6 = f32[4,2,64,1536]{3,2,0,1:T(8,128)} fusion(bf16[2,1024,1536]{2,1,0:T(8,128)(2,1)} %param.7, bf16[4,2,64,1024]{3,2,1,0:T(8,128)(2,1)S(1)} %all_to_all.10), kind=kOutput, calls=%fused_computation.9 | convolution fusion | flops 1610612736 | bytes 10485760 | tf_op jit(solution)/shard_map/sjnd,jdf->sjnf/dot_general | solution.py:30
  39.4 0.0 reduce-scatter.3.cloned.1.call-update
  39.5 0.0 reduce-scatter.5.cloned.1.call-start
  39.5 6.3 %fusion.9 = f32[4,2,64,1536]{3,2,0,1:T(8,128)} fusion(bf16[2,1024,1536]{2,1,0:T(8,128)(2,1)} %param.8, bf16[4,2,64,1024]{3,2,1,0:T(8,128)(2,1)S(1)} %all_to_all.10), kind=kOutput, calls=%fused_computation.10 | convolution fusion | flops 1610612736 | bytes 10485760 | tf_op jit(solution)/shard_map/sjnd,jdf->sjnf/dot_general | solution.py:31
  45.8 0.0 reduce-scatter.5.cloned.1.call-update
  45.8 0.0 all-gather.2.cloned.1.call-start
  45.9 54.4 %reduce-scatter.3.cloned.1.call-done = f32[4,2,64,384]{3,2,0,1:T(8,128)} async-done(((f32[4,2,64,1536]{3,2,0,1:T(8,128)}), f32[4,2,64,384]{3,2,0,1:T(8,128)}) %reduce-scatter.3.cloned.1.call-update) | async-done | bytes 786448 | tf_op jit(solution)/shard_map/reduce_scatter | solution.py:32
  100.3 62.6 %reduce-scatter.5.cloned.1.call-done = f32[4,2,64,384]{3,2,0,1:T(8,128)} async-done(((f32[4,2,64,1536]{3,2,0,1:T(8,128)}), f32[4,2,64,384]{3,2,0,1:T(8,128)}) %reduce-scatter.5.cloned.1.call-update) | async-done | bytes 786448 | tf_op jit(solution)/shard_map/reduce_scatter | solution.py:33
  163.0 2.3 multiply_convert_fusion
  165.3 0.0 all-gather.2.cloned.1.call-update
  165.3 0.0 copy-start.1
  165.3 36.7 %all-gather.2.cloned.1.call-done = bf16[4,2,64,1536]{3,2,0,1:T(8,128)(2,1)} async-done(((bf16[4,2,64,384]{3,2,0,1:T(8,128)(2,1)}), bf16[4,2,64,1536]{3,2,0,1:T(8,128)(2,1)}) %all-gather.2.cloned.1.call-update) | async-done | bytes 1572880 | tf_op jit(solution)/shard_map/all_gather | solution.py:35
  202.0 5.1 %fusion.16 = bf16[4,2,64,1024]{3,2,0,1:T(8,128)(2,1)S(1)} fusion(bf16[4,2,64,1536]{3,2,0,1:T(8,128)(2,1)} %all-gather.2.cloned.1.call-done, bf16[2,1536,1024]{2,1,0:T(8,128)(2,1)} %param.9), kind=kOutput, calls=%fused_computation.14 | convolution fusion | flops 1611137024 | bytes 8912896 | tf_op jit(solution)/shard_map/sjnf,jfd->sjnd/dot_general | solution.py:36
  207.1 1.1 copy.20
  208.1 3.5 %all-to-all-start.1 = ((bf16[4,2,64,1024]{3,2,1,0:T(8,128)(2,1)}), bf16[4,2,64,1024]{3,2,1,0:T(8,128)(2,1)S(1)}, u32[]{:S(2)}, u32[]{:S(2)}) async-start(bf16[4,2,64,1024]{3,2,1,0:T(8,128)(2,1)} %copy.20), calls=%async_computation.3 | async-start | bytes 2097152 | tf_op jit(solution)/shard_map/all_to_all | solution.py:38
  211.7 0.0 copy-done.1
  211.7 0.1 copy.21
  211.8 14.3 %all-to-all-done.1 = bf16[4,2,64,1024]{3,2,1,0:T(8,128)(2,1)S(1)} async-done(((bf16[4,2,64,1024]{3,2,1,0:T(8,128)(2,1)}), bf16[4,2,64,1024]{3,2,1,0:T(8,128)(2,1)S(1)}, u32[]{:S(2)}, u32[]{:S(2)}) %all-to-all-start.1) | async-done | bytes 1048608 | tf_op jit(solution)/shard_map/all_to_all | solution.py:38
  226.1 2.0 gather_fusion.1
  228.1 1.4 fusion.12
  (9 shorter events, 0.1 us)
Async XLA Ops:
  6.5 6.0 %copy-start = (bf16[64,1024]{1,0:T(8,128)(2,1)S(1)}, bf16[64,1024]{1,0:T(8,128)(2,1)}, u32[]{:S(2)}) copy-start(bf16[64,1024]{1,0:T(8,128)(2,1)} %param.6) | copy-start | bytes 393220
  6.5 93.8 %reduce-scatter.3.cloned.1.call-start = ((), (), s32[]{:S(2)}) async-start(), calls=%async_computation.4 | async-start | bytes 3932160 | tf_op jit(solution)/shard_map/reduce_scatter | solution.py:32
  39.5 123.5 %reduce-scatter.5.cloned.1.call-start = ((), (), s32[]{:S(2)}) async-start(), calls=%async_computation.5 | async-start | bytes 3932160 | tf_op jit(solution)/shard_map/reduce_scatter | solution.py:33
  45.8 156.2 %all-gather.2.cloned.1.call-start = ((), (), s32[]{:S(2)}) async-start(), calls=%async_computation.6 | async-start | bytes 1966080 | tf_op jit(solution)/shard_map/all_gather | solution.py:35
  165.3 46.3 %copy-start.1 = (f32[64,8]{0,1:T(8,128)S(1)}, f32[64,8]{0,1:T(8,128)}, u32[]{:S(2)}) copy-start(f32[64,8]{0,1:T(8,128)} %param.11) | copy-start | bytes 6148
  208.1 17.9 %all-to-all-start.1 = ((bf16[4,2,64,1024]{3,2,1,0:T(8,128)(2,1)}), bf16[4,2,64,1024]{3,2,1,0:T(8,128)(2,1)S(1)}, u32[]{:S(2)}, u32[]{:S(2)}) async-start(bf16[4,2,64,1024]{3,2,1,0:T(8,128)(2,1)} %copy.20), calls=%async_computation.3 | async-start | bytes 2097152 | tf_op jit(solution)/shard_map/all_to_all | solution.py:38
Sparse Core Ops, SparseCore 0:
  39.6 60.6 reduce-scatter.2
  102.6 60.3 reduce-scatter.4
  165.4 36.5 all-gather.1
where the time goes:
time: 236 us
  waiting for transfers between devices  168 us (71%)
  blocking collectives  18.5 us (8%)
  matrix products  17.6 us (7%)
  between operations  13.2 us (6%)
  local copies, waits for them, and re-layouts  9.18 us (4%)
  other arithmetic  5.83 us (2%)
  starting transfers between devices  3.6 us (2%)
    reduce_scatter x1, waiting for transfers between devices, per_device(): lax.psum_scatter(up_part, 'tensor', scatter_dimension=3, tiled=True)  62.6 us
    reduce_scatter x1, waiting for transfers between devices, per_device(): lax.psum_scatter(gate_part, 'tensor', scatter_dimension=3, tiled=True)  54.4 us
    all_gather x1, waiting for transfers between devices, per_device(): hidden = lax.all_gather(hidden_share, 'tensor', axis=3, tiled=True)  36.7 us
    all_to_all x1, blocking collectives, per_device(): lax.all_to_all(outgoing, 'expert', split_axis=0, concat_axis=0, tiled=True)  18.5 us
    all_to_all x1, waiting for transfers between devices, per_device(): lax.all_to_all(returned, 'expert', split_axis=0, concat_axis=0, tiled=True)  14.3 us
    dot_general x1, matrix products, per_device(): jnp.einsum('sjnd,jdf->sjnf', received, w_up, preferred_element_type=jnp.f...  6.3 us
    dot_general x1, matrix products, per_device(): jnp.einsum('sjnd,jdf->sjnf', received, w_gate, preferred_element_type=jnp...  6.27 us
    dot_general x1, matrix products, per_device(): jnp.einsum('sjnf,jfd->sjnd', hidden, w_down, preferred_element_type=jnp.f...  5.06 us
  transfers between devices with their start and end apart: 4, of which 4 were waited for; matrix products, arithmetic and copies ran while one was open for 3% of the time, Pallas kernels for 0%

commit v1 on v0

--- a/solution.py
+++ b/solution.py
@@ -32,8 +32,38 @@
     gate_share = lax.psum_scatter(gate_part, "tensor", scatter_dimension=3, tiled=True)
     up_share = lax.psum_scatter(up_part, "tensor", scatter_dimension=3, tiled=True)
     hidden_share = (jax.nn.silu(gate_share) * up_share).astype(jnp.bfloat16)
-    hidden = lax.all_gather(hidden_share, "tensor", axis=3, tiled=True)
-    result = jnp.einsum("sjnf,jfd->sjnd", hidden, w_down, preferred_element_type=jnp.float32)
+    size, index, width = (lax.axis_size("tensor"), lax.axis_index("tensor"), hidden_share.shape[3])
+    right = [(i, (i + 1) % size) for i in range(size)]
+    left = [(i, (i - 1) % size) for i in range(size)]
+    half = size // 2
+    from_left = from_right = hidden_share
+    running = jnp.einsum(
+        "sjnf,jfd->sjnd",
+        hidden_share,
+        lax.dynamic_slice_in_dim(w_down, index * width, hidden_share.shape[3], axis=1),
+        preferred_element_type=jnp.float32,
+    )
+    for hop in range(1, half + 1):
+        from_left = lax.ppermute(from_left, "tensor", right)
+        if hop < size - half:
+            from_right = lax.ppermute(from_right, "tensor", left)
+            running = running + jnp.einsum(
+                "sjnf,jfd->sjnd",
+                from_right,
+                lax.dynamic_slice_in_dim(
+                    w_down, (index + hop) % size * width, from_right.shape[3], axis=1
+                ),
+                preferred_element_type=jnp.float32,
+            )
+        running = running + jnp.einsum(
+            "sjnf,jfd->sjnd",
+            from_left,
+            lax.dynamic_slice_in_dim(
+                w_down, (index - hop) % size * width, from_left.shape[3], axis=1
+            ),
+            preferred_element_type=jnp.float32,
+        )
+    result = running
     returned = result.astype(jnp.bfloat16)
     combined = lax.all_to_all(returned, "expert", split_axis=0, concat_axis=0, tiled=True).reshape(
         experts_all * capacity, col_share

time: 236 us -> 224 us (0.949)
  waiting for transfers between devices: 168 us -> 146 us
  starting transfers between devices: 3.6 us -> 12.9 us
    all_gather x1 -> x0, waiting for transfers between devices: 36.7 us -> none  [per_device(): hidden = lax.all_gather(hidden_share, 'tensor', axis=3, tiled=True)]
    ppermute x0 -> x3, waiting for transfers between devices: none -> 14.8 us  [the longest x2 14.8 us: per_device(): from_left = lax.ppermute(from_left, 'tensor', right)]
    ppermute x0 -> x3, starting transfers between devices: none -> 9.34 us  [the longest x2 6.39 us: per_device(): from_left = lax.ppermute(from_left, 'tensor', right)]
    dot_general x1 -> x4, matrix products: 5.06 us -> 5.75 us  [the longest x2 2.9 us: per_device(): jnp.einsum('sjnf,jfd->sjnd', from_left, lax.dynamic_slice_in_dim(w_down,...]
  transfers between devices with their start and end apart: 4 -> 6, of which waited for: 4 -> 5; matrix products, arithmetic and copies ran while one was open for 3% -> 5% of each run, Pallas kernels for 0% -> 0%
where the time goes in v1:
time: 224 us
  waiting for transfers between devices  146 us (65%)
  blocking collectives  18.5 us (8%)
  matrix products  18.3 us (8%)
  between operations  13.6 us (6%)
  starting transfers between devices  12.9 us (6%)
  local copies, waits for them, and re-layouts  9.21 us (4%)
  other arithmetic  5.23 us (2%)
    reduce_scatter x1, waiting for transfers between devices, per_device(): lax.psum_scatter(up_part, 'tensor', scatter_dimension=3, tiled=True)  62.6 us
    reduce_scatter x1, waiting for transfers between devices, per_device(): lax.psum_scatter(gate_part, 'tensor', scatter_dimension=3, tiled=True)  54.5 us
    all_to_all x1, blocking collectives, per_device(): lax.all_to_all(outgoing, 'expert', split_axis=0, concat_axis=0, tiled=True)  18.5 us
    ppermute x2, waiting for transfers between devices, per_device(): from_left = lax.ppermute(from_left, 'tensor', right)  14.8 us
    all_to_all x1, waiting for transfers between devices, per_device(): lax.all_to_all(returned, 'expert', split_axis=0, concat_axis=0, tiled=True)  14.3 us
    ppermute x2, starting transfers between devices, per_device(): from_left = lax.ppermute(from_left, 'tensor', right)  6.39 us
    dot_general x1, matrix products, per_device(): jnp.einsum('sjnd,jdf->sjnf', received, w_up, preferred_element_type=jnp.f...  6.28 us
    dot_general x1, matrix products, per_device(): jnp.einsum('sjnd,jdf->sjnf', received, w_gate, preferred_element_type=jnp...  6.24 us
  transfers between devices with their start and end apart: 6, of which 5 were waited for; matrix products, arithmetic and copies ran while one was open for 5% of the time, Pallas kernels for 0%

profile of v1, /device:TPU:0, one launch (start us, length us, event | category | flops | bytes accessed | tf_op | source)
XLA Modules:
  0.0 224.0 jit_solution(14919345677644659345)
XLA Ops:
  6.5 0.0 copy-start
  6.5 0.0 reduce-scatter.3.cloned.1.call-start
  6.5 0.8 copy.16
  7.3 0.1 eq.33
  7.4 0.1 eq.29
  7.5 0.7 broadcast_multiply_fusion
  8.2 1.1 reduce-window.6
  9.4 0.2 slice_reduce_fusion
  9.6 0.1 copy.15
  9.7 0.1 mul.45
  9.8 0.1 fusion.28
  9.9 2.4 %scatter_custom_fusion = s32[512]{0:T(512)S(1)} fusion(s32[512]{0:T(512)S(1)} %bitcast.65, s32[512]{0:T(512)S(1)} %add_select_fusion, s32[]{:T(128)} %constant.58.clone.1), kind=kCustom, calls=%fused_computation.48 | custom fusion | bytes 2052 | tf_op jit(solution)/shard_map/scatter | solution.py:25
  12.4 0.1 broadcast_in_dim.26
  12.5 0.0 copy-done
  12.5 2.1 gather_fusion
  14.5 0.1 broadcast_select_fusion
  14.7 18.5 %all_to_all.10 = bf16[4,2,64,1024]{3,2,1,0:T(8,128)(2,1)S(1)} all-to-all(bf16[4,2,64,1024]{3,2,1,0:T(8,128)(2,1)S(1)} %broadcast_select_fusion), channel_id=1, replica_groups=mesh['group'=2,'expert'=4,'tensor'=4] {'expert'}, dimensions={0} | all-to-all | bytes 2097152 | tf_op jit(solution)/shard_map/all_to_all | solution.py:29
  33.2 6.2 %fusion.4 = f32[4,2,64,1536]{3,2,0,1:T(8,128)} fusion(bf16[2,1024,1536]{2,1,0:T(8,128)(2,1)} %param.7, bf16[4,2,64,1024]{3,2,1,0:T(8,128)(2,1)S(1)} %all_to_all.10), kind=kOutput, calls=%fused_computation.7 | convolution fusion | flops 1610612736 | bytes 10485760 | tf_op jit(solution)/shard_map/sjnd,jdf->sjnf/dot_general | solution.py:30
  39.4 0.0 reduce-scatter.3.cloned.1.call-update
  39.4 0.0 reduce-scatter.5.cloned.1.call-start
  39.5 6.3 %fusion.7 = f32[4,2,64,1536]{3,2,0,1:T(8,128)} fusion(bf16[2,1024,1536]{2,1,0:T(8,128)(2,1)} %param.8, bf16[4,2,64,1024]{3,2,1,0:T(8,128)(2,1)S(1)} %all_to_all.10), kind=kOutput, calls=%fused_computation.8 | convolution fusion | flops 1610612736 | bytes 10485760 | tf_op jit(solution)/shard_map/sjnd,jdf->sjnf/dot_general | solution.py:31
  45.8 0.0 reduce-scatter.5.cloned.1.call-update
  45.8 54.5 %reduce-scatter.3.cloned.1.call-done = f32[4,2,64,384]{3,2,0,1:T(8,128)} async-done(((f32[4,2,64,1536]{3,2,0,1:T(8,128)}), f32[4,2,64,384]{3,2,0,1:T(8,128)}) %reduce-scatter.3.cloned.1.call-update) | async-done | bytes 786448 | tf_op jit(solution)/shard_map/reduce_scatter | solution.py:32
  100.3 62.6 %reduce-scatter.5.cloned.1.call-done = f32[4,2,64,384]{3,2,0,1:T(8,128)} async-done(((f32[4,2,64,1536]{3,2,0,1:T(8,128)}), f32[4,2,64,384]{3,2,0,1:T(8,128)}) %reduce-scatter.5.cloned.1.call-update) | async-done | bytes 786448 | tf_op jit(solution)/shard_map/reduce_scatter | solution.py:33
  163.0 0.0 slice-start
  163.0 1.7 multiply_convert_fusion
  164.7 0.9 collective-permute-start.1
  165.6 0.0 slice-start.1
  165.6 2.9 %collective-permute-start = (bf16[4,2,64,384]{3,2,0,1:T(8,128)(2,1)S(1)}, bf16[4,2,64,384]{3,2,0,1:T(8,128)(2,1)S(1)}, u32[]{:S(2)}, u32[]{:S(2)}) collective-permute-start(bf16[4,2,64,384]{3,2,0,1:T(8,128)(2,1)S(1)} %multiply_convert_fusion), channel_id=1, source_target_pairs={{0,3},{1,0},{2,1},{3,2},{4,7},{5,4},{6,5},{7,6},{8,11},{9,8},{10,9... | collective-permute-start | bytes 1179656 | tf_op jit(solution)/shard_map/ppermute | solution.py:49
  168.6 2.1 fusion.16
  170.7 7.9 %collective-permute-done.1 = bf16[4,2,64,384]{3,2,0,1:T(8,128)(2,1)S(1)} collective-permute-done((bf16[4,2,64,384]{3,2,0,1:T(8,128)(2,1)S(1)}, bf16[4,2,64,384]{3,2,0,1:T(8,128)(2,1)S(1)}, u32[]{:S(2)}, u32[]{:S(2)}) %collective-permute-start.1) | collective-permute-done | bytes 393248 | tf_op jit(solution)/shard_map/ppermute | solution.py:47
  178.6 5.5 %collective-permute-start.2 = (bf16[4,2,64,384]{3,2,0,1:T(8,128)(2,1)S(1)}, bf16[4,2,64,384]{3,2,0,1:T(8,128)(2,1)S(1)}, u32[]{:S(2)}, u32[]{:S(2)}) collective-permute-start(bf16[4,2,64,384]{3,2,0,1:T(8,128)(2,1)S(1)} %collective-permute-done.1), channel_id=1, source_target_pairs={{0,1},{1,2},{2,3},{3,0},{4,5},{5,6},{6,7},{7,4},{8,9},{9,10},{10,1... | collective-permute-start | bytes 1179656 | tf_op jit(solution)/shard_map/ppermute | solution.py:47
  184.1 2.1 fusion.12
  186.2 0.0 collective-permute-done
  186.2 0.0 slice-done
  186.2 0.0 slice-done.1
  186.2 0.7 fusion.14
  187.0 6.9 %collective-permute-done.2 = bf16[4,2,64,384]{3,2,0,1:T(8,128)(2,1)S(1)} collective-permute-done((bf16[4,2,64,384]{3,2,0,1:T(8,128)(2,1)S(1)}, bf16[4,2,64,384]{3,2,0,1:T(8,128)(2,1)S(1)}, u32[]{:S(2)}, u32[]{:S(2)}) %collective-permute-start.2) | collective-permute-done | bytes 393248 | tf_op jit(solution)/shard_map/ppermute | solution.py:47
  193.9 0.8 fusion.22
  194.7 0.0 copy-start.1
  194.7 1.1 copy.20
  195.8 3.5 %all-to-all-start.1 = ((bf16[4,2,64,1024]{3,2,1,0:T(8,128)(2,1)}), bf16[4,2,64,1024]{3,2,1,0:T(8,128)(2,1)S(1)}, u32[]{:S(2)}, u32[]{:S(2)}) async-start(bf16[4,2,64,1024]{3,2,1,0:T(8,128)(2,1)} %copy.20), calls=%async_computation.3 | async-start | bytes 2097152 | tf_op jit(solution)/shard_map/all_to_all | solution.py:68
  199.3 0.0 copy-done.1
  199.4 0.1 copy.21
  199.4 14.3 %all-to-all-done.1 = bf16[4,2,64,1024]{3,2,1,0:T(8,128)(2,1)S(1)} async-done(((bf16[4,2,64,1024]{3,2,1,0:T(8,128)(2,1)}), bf16[4,2,64,1024]{3,2,1,0:T(8,128)(2,1)S(1)}, u32[]{:S(2)}, u32[]{:S(2)}) %all-to-all-start.1) | async-done | bytes 1048608 | tf_op jit(solution)/shard_map/all_to_all | solution.py:68
  213.7 2.0 gather_fusion.1
  215.8 1.3 fusion.10
  (10 shorter events, 0.1 us)
Async XLA Ops:
  6.5 6.0 %copy-start = (bf16[64,1024]{1,0:T(8,128)(2,1)S(1)}, bf16[64,1024]{1,0:T(8,128)(2,1)}, u32[]{:S(2)}) copy-start(bf16[64,1024]{1,0:T(8,128)(2,1)} %param.6) | copy-start | bytes 393220
  6.5 93.8 %reduce-scatter.3.cloned.1.call-start = ((), (), s32[]{:S(2)}) async-start(), calls=%async_computation.4 | async-start | bytes 3932160 | tf_op jit(solution)/shard_map/reduce_scatter | solution.py:32
  39.4 123.5 %reduce-scatter.5.cloned.1.call-start = ((), (), s32[]{:S(2)}) async-start(), calls=%async_computation.5 | async-start | bytes 3932160 | tf_op jit(solution)/shard_map/reduce_scatter | solution.py:33
  163.0 23.2 %slice-start = ((s8[6291456]{0:T(1024)(128)(4,1)}), s8[2097152]{0:T(1024)(128)(4,1)S(1)}, s32[]{:S(2)}) async-start(s8[6291456]{0:T(1024)(128)(4,1)} %bitcast.62), calls=%async_computation.6 | async-start | bytes 4194304
  164.7 13.9 %collective-permute-start.1 = (bf16[4,2,64,384]{3,2,0,1:T(8,128)(2,1)S(1)}, bf16[4,2,64,384]{3,2,0,1:T(8,128)(2,1)S(1)}, u32[]{:S(2)}, u32[]{:S(2)}) collective-permute-start(bf16[4,2,64,384]{3,2,0,1:T(8,128)(2,1)S(1)} %multiply_convert_fusion), channel_id=1, source_target_pairs={{0,1},{1,2},{2,3},{3,0},{4,5},{5,6},{6,7},{7,4},{8,9},{9,10},{10,1... | collective-permute-start | bytes 1179656 | tf_op jit(solution)/shard_map/ppermute | solution.py:47
  165.6 20.6 %slice-start.1 = ((s8[6291456]{0:T(1024)(128)(4,1)}), s8[4194304]{0:T(1024)(128)(4,1)S(1)}, s32[]{:S(2)}) async-start(s8[6291456]{0:T(1024)(128)(4,1)} %bitcast.62), calls=%async_computation.7 | async-start | bytes 8388608
  165.6 20.5 %collective-permute-start = (bf16[4,2,64,384]{3,2,0,1:T(8,128)(2,1)S(1)}, bf16[4,2,64,384]{3,2,0,1:T(8,128)(2,1)S(1)}, u32[]{:S(2)}, u32[]{:S(2)}) collective-permute-start(bf16[4,2,64,384]{3,2,0,1:T(8,128)(2,1)S(1)} %multiply_convert_fusion), channel_id=1, source_target_pairs={{0,3},{1,0},{2,1},{3,2},{4,7},{5,4},{6,5},{7,6},{8,11},{9,8},{10,9... | collective-permute-start | bytes 1179656 | tf_op jit(solution)/shard_map/ppermute | solution.py:49
  178.6 15.3 %collective-permute-start.2 = (bf16[4,2,64,384]{3,2,0,1:T(8,128)(2,1)S(1)}, bf16[4,2,64,384]{3,2,0,1:T(8,128)(2,1)S(1)}, u32[]{:S(2)}, u32[]{:S(2)}) collective-permute-start(bf16[4,2,64,384]{3,2,0,1:T(8,128)(2,1)S(1)} %collective-permute-done.1), channel_id=1, source_target_pairs={{0,1},{1,2},{2,3},{3,0},{4,5},{5,6},{6,7},{7,4},{8,9},{9,10},{10,1... | collective-permute-start | bytes 1179656 | tf_op jit(solution)/shard_map/ppermute | solution.py:47
  194.7 4.6 %copy-start.1 = (f32[64,8]{0,1:T(8,128)S(1)}, f32[64,8]{0,1:T(8,128)}, u32[]{:S(2)}) copy-start(f32[64,8]{0,1:T(8,128)} %param.11) | copy-start | bytes 6148
  195.8 17.9 %all-to-all-start.1 = ((bf16[4,2,64,1024]{3,2,1,0:T(8,128)(2,1)}), bf16[4,2,64,1024]{3,2,1,0:T(8,128)(2,1)S(1)}, u32[]{:S(2)}, u32[]{:S(2)}) async-start(bf16[4,2,64,1024]{3,2,1,0:T(8,128)(2,1)} %copy.20), calls=%async_computation.3 | async-start | bytes 2097152 | tf_op jit(solution)/shard_map/all_to_all | solution.py:68
Sparse Core Ops, SparseCore 0:
  39.6 60.7 reduce-scatter.2
  102.6 60.3 reduce-scatter.4
